TPU v7x, 32 devices: a whole 2x2x4 slice. The times are simulated.
32 devices in a mesh: sweep: 1, dp: 8 (over z, y), tensor: 4 (over x, core).
Axes of the slice: x: 2, y: 2, z: 4, core: 2. Of those that a mesh axis runs over, the one named last changes fastest.
Arguments:
- checkpoint: bfloat16 [1024, 8192], P(('sweep', 'dp'), 'tensor'), may hold values from -6 to 6
- norm_gain: bfloat16 [8192], P(('sweep', 'tensor')), may hold values from 0.5 to 1.5
- w_query: bfloat16 [8192, 4096], P(('sweep', 'dp'), 'tensor'), may hold values from -1 to 1
- w_key: bfloat16 [8192, 512], P(('sweep', 'dp'), 'tensor'), may hold values from -8 to 8
- w_value: bfloat16 [8192, 512], P(('sweep', 'dp'), 'tensor'), may hold values from -0.0625 to 0.0625
- grad_attn: bfloat16 [1024, 4096], P(('sweep', 'dp'), 'tensor'), may hold values from -6 to 6
Outputs:
- d_checkpoint: bfloat16 [1024, 8192], P(('sweep', 'dp'), 'tensor')
- grad_gain: float32 [8192], P(('sweep', 'tensor'))
- grad_query: float32 [8192, 4096], P(('sweep', 'dp'), 'tensor')
- grad_key: float32 [8192, 512], P(('sweep', 'dp'), 'tensor')
- grad_value: float32 [8192, 512], P(('sweep', 'dp'), 'tensor')
All inputs are finite; a program needn't handle non-finite values.
Results may differ from a plain program's by a relative error of at most 0.025.
The roundings to bfloat16 on the way count: a program that leaves them out, or rounds other values in their place, can miss the bound.
Values may be sent and summed in bfloat16 or wider, within the bound.
A program may use at most 128 MiB of HBM per device.

v0:
```python
import jax
import jax.numpy as jnp
from jax import lax
from jax.sharding import PartitionSpec as P

QHEADS = 32
KVHEADS = 4
HD = 128


EPS = 1e-05
THETA = 500000.0


def round_half(field):
    return lax.optimization_barrier(field.astype(jnp.bfloat16))


def angles(positions, head_width):
    frequency = THETA ** (-(jnp.arange(head_width // 2, dtype=jnp.float32) * 2.0) / head_width)
    turned = positions.astype(jnp.float32)[:, None] * frequency[None, :]
    return (jnp.cos(turned)[:, None, :], jnp.sin(turned)[:, None, :])


def rotate(field, cosine_table, sine_table):
    half_width = field.shape[-1] // 2
    front_half = field[..., :half_width]
    back_half = field[..., half_width:]
    return jnp.concatenate(
        [
            front_half * cosine_table - back_half * sine_table,
            back_half * cosine_table + front_half * sine_table,
        ],
        -1,
    )


def rotate_back(field, cosine_table, sine_table):
    half_width = field.shape[-1] // 2
    front_half = field[..., :half_width]
    back_half = field[..., half_width:]
    return jnp.concatenate(
        [
            front_half * cosine_table + back_half * sine_table,
            back_half * cosine_table - front_half * sine_table,
        ],
        -1,
    )


def project_back(grads, matrix):
    return jnp.einsum("tc,dc->td", grads, matrix, preferred_element_type=jnp.float32)


def on_device(checkpoint, norm_gain, w_query, w_key, w_value, grad_attn):
    row_count = checkpoint.shape[0]
    head_width = HD
    group_size = QHEADS // KVHEADS
    full_x, full_gain = (
        lax.all_gather(checkpoint, "tensor", axis=1, tiled=True),
        lax.all_gather(norm_gain, "tensor", axis=0, tiled=True),
    )
    x_wide = full_x.astype(jnp.float32)
    gain_wide = full_gain.astype(jnp.float32)
    model_width = full_x.shape[1]
    inverse = lax.rsqrt(jnp.mean(x_wide * x_wide, -1, keepdims=True) + EPS)
    normed = (x_wide * inverse * gain_wide).astype(jnp.bfloat16)
    query_all, key_all, value_all = (
        lax.all_gather(w_query, "dp", axis=0, tiled=True),
        lax.all_gather(w_key, "dp", axis=0, tiled=True),
        lax.all_gather(w_value, "dp", axis=0, tiled=True),
    )
    q_heads = query_all.shape[1] // head_width
    own_kv = max(1, q_heads // group_size)
    run_heads = q_heads // own_kv
    first_kv = lax.axis_index("tensor") * q_heads // group_size
    queries = jnp.dot(normed, query_all, preferred_element_type=jnp.float32).reshape(
        row_count, q_heads, head_width
    )
    key_local = jnp.dot(normed, key_all, preferred_element_type=jnp.float32)
    value_local = jnp.dot(normed, value_all, preferred_element_type=jnp.float32)
    key_cols_all, value_cols_all = (
        lax.all_gather(key_local, "tensor", axis=1, tiled=True),
        lax.all_gather(value_local, "tensor", axis=1, tiled=True),
    )
    kv_total = key_cols_all.shape[1] // head_width
    first_row = lax.axis_index("dp") * row_count
    own_positions = first_row + jnp.arange(row_count, dtype=jnp.int32)
    cosine_table, sine_table = angles(own_positions, head_width)
    query_rot = rotate(queries, cosine_table, sine_table).astype(jnp.bfloat16)
    key_heads = lax.dynamic_slice_in_dim(
        key_cols_all.reshape(row_count, head_width, kv_total), first_kv, own_kv, 2
    )
    value_heads = lax.dynamic_slice_in_dim(
        value_cols_all.reshape(row_count, head_width, kv_total), first_kv, own_kv, 2
    )
    key_turned = rotate(jnp.transpose(key_heads, (0, 2, 1)), cosine_table, sine_table)
    key_rot = key_turned.astype(jnp.bfloat16).reshape(row_count, own_kv * head_width)
    value_half = (
        jnp.transpose(value_heads, (0, 2, 1))
        .astype(jnp.bfloat16)
        .reshape(row_count, own_kv * head_width)
    )
    gathered_keys, gathered_values = (
        lax.all_gather(key_rot, "dp", axis=0, tiled=True),
        lax.all_gather(value_half, "dp", axis=0, tiled=True),
    )
    seq_length = gathered_keys.shape[0]
    keys_three = gathered_keys.reshape(seq_length, own_kv, head_width)
    values_three = gathered_values.reshape(seq_length, own_kv, head_width)
    score_scale = head_width ** (-0.5)
    query_grp = query_rot.reshape(row_count, own_kv, run_heads, head_width)
    upstream = grad_attn.reshape(row_count, own_kv, run_heads, head_width)
    scores = (
        jnp.einsum("tkgd,skd->kgts", query_grp, keys_three, preferred_element_type=jnp.float32)
        * score_scale
    )
    allowed = own_positions[:, None] >= jnp.arange(seq_length, dtype=jnp.int32)[None, :]
    scores = jnp.where(allowed, scores, -jnp.inf)
    row_top = jnp.max(scores, -1, keepdims=True)
    raw_weights = jnp.exp(scores - row_top)
    chances = raw_weights / jnp.sum(raw_weights, -1, keepdims=True)
    chances_half = chances.astype(jnp.bfloat16)
    attended = jnp.einsum(
        "kgts,skd->tkgd", chances_half, values_three, preferred_element_type=jnp.float32
    )
    row_delta = jnp.sum(upstream.astype(jnp.float32) * attended, -1)
    prob_grads = jnp.einsum(
        "tkgd,skd->kgts", upstream, values_three, preferred_element_type=jnp.float32
    )
    dscore = chances * (prob_grads - jnp.transpose(row_delta, (1, 2, 0))[..., None])
    dscore_half = dscore.astype(jnp.bfloat16)
    dquery = (
        jnp.einsum("kgts,skd->tkgd", dscore_half, keys_three, preferred_element_type=jnp.float32)
        * score_scale
    )
    dkey_part = (
        jnp.einsum("kgts,tkgd->skd", dscore_half, query_grp, preferred_element_type=jnp.float32)
        * score_scale
    )
    dvalue_part = jnp.einsum(
        "kgts,tkgd->skd", chances_half, upstream, preferred_element_type=jnp.float32
    )
    dkey_sum, dvalue_sum = (
        lax.psum_scatter(
            dkey_part.reshape(seq_length, own_kv * head_width).astype(jnp.bfloat16),
            "dp",
            scatter_dimension=0,
            tiled=True,
        ).astype(jnp.float32),
        lax.psum_scatter(
            dvalue_part.reshape(seq_length, own_kv * head_width).astype(jnp.bfloat16),
            "dp",
            scatter_dimension=0,
            tiled=True,
        ).astype(jnp.float32),
    )
    dkey_back = rotate_back(
        dkey_sum.reshape(row_count, own_kv, head_width), cosine_table, sine_table
    )
    dvalue_back = dvalue_sum.reshape(row_count, own_kv, head_width)
    empty_heads = jnp.zeros((row_count, kv_total, head_width), jnp.float32)
    zero_start = jnp.zeros((), jnp.int32)
    dkey_embed = lax.dynamic_update_slice(
        empty_heads, dkey_back, (zero_start, first_kv, zero_start)
    )
    dvalue_embed = lax.dynamic_update_slice(
        empty_heads, dvalue_back, (zero_start, first_kv, zero_start)
    )
    dkey_embed = jnp.transpose(dkey_embed, (0, 2, 1)).reshape(row_count, head_width * kv_total)
    dvalue_embed = jnp.transpose(dvalue_embed, (0, 2, 1)).reshape(row_count, head_width * kv_total)
    dkey_cols, dvalue_cols = (
        lax.psum_scatter(
            dkey_embed.astype(jnp.bfloat16), "tensor", scatter_dimension=1, tiled=True
        ).astype(jnp.float32),
        lax.psum_scatter(
            dvalue_embed.astype(jnp.bfloat16), "tensor", scatter_dimension=1, tiled=True
        ).astype(jnp.float32),
    )
    dquery_pre = (
        rotate_back(dquery.reshape(row_count, q_heads, head_width), cosine_table, sine_table)
        .astype(jnp.bfloat16)
        .reshape(row_count, q_heads * head_width)
    )
    dkey_pre = dkey_cols.astype(jnp.bfloat16)
    dvalue_pre = dvalue_cols.astype(jnp.bfloat16)
    partial_input = (
        project_back(dquery_pre, query_all)
        + project_back(dkey_pre, key_all)
        + project_back(dvalue_pre, value_all)
    )
    slice_width = checkpoint.shape[1]
    x_own = checkpoint.astype(jnp.float32)
    gain_own = norm_gain.astype(jnp.float32)
    input_full = lax.psum(partial_input.astype(jnp.bfloat16), "tensor").astype(jnp.float32)
    row_sum = jnp.sum(gain_wide * input_full * x_wide, -1, keepdims=True)
    input_own = lax.dynamic_slice_in_dim(
        input_full, lax.axis_index("tensor") * slice_width, slice_width, 1
    )
    d_checkpoint = (
        inverse * gain_own * input_own - x_own * inverse**3 * row_sum / model_width
    ).astype(jnp.bfloat16)
    grad_gain = lax.psum(jnp.sum(input_own * x_own * inverse, 0), "dp")
    token_grads = jnp.concatenate([dquery_pre, dkey_pre, dvalue_pre], 1)
    own_rows = w_query.shape[0]
    feature_cols = lax.all_to_all(normed, "dp", split_axis=1, concat_axis=0, tiled=True)
    piece = lax.all_gather(token_grads, "dp", axis=0, tiled=True)
    piece_rows = piece.shape[0]
    blocks = piece_rows // row_count
    block_x = feature_cols.reshape(blocks, row_count, own_rows)
    block_g = piece.reshape(blocks, row_count, piece.shape[1])
    terms = jnp.einsum("btd,btc->bdc", block_x, block_g, preferred_element_type=jnp.float32)
    weight_grads = jnp.sum(round_half(terms).astype(jnp.float32), 0)
    query_cols = w_query.shape[1]
    key_cols = w_key.shape[1]
    grad_query = weight_grads[:, :query_cols]
    grad_key = weight_grads[:, query_cols : query_cols + key_cols]
    grad_value = weight_grads[:, query_cols + key_cols :]
    return (d_checkpoint, grad_gain, grad_query, grad_key, grad_value)


def solution(mesh):
    return jax.shard_map(
        on_device,
        mesh=mesh,
        in_specs=(
            P(("sweep", "dp"), "tensor"),
            P(("sweep", "tensor")),
            P(("sweep", "dp"), "tensor"),
            P(("sweep", "dp"), "tensor"),
            P(("sweep", "dp"), "tensor"),
            P(("sweep", "dp"), "tensor"),
        ),
        out_specs=(
            P(("sweep", "dp"), "tensor"),
            P(("sweep", "tensor")),
            P(("sweep", "dp"), "tensor"),
            P(("sweep", "dp"), "tensor"),
            P(("sweep", "dp"), "tensor"),
        ),
        check_vma=False,
    )
```

profile of v0, /device:TPU:0, one launch (start us, length us, event | category | flops | bytes accessed | tf_op | source)
XLA Modules:
  0.0 710.5 jit_solution(5812037475579603408)
XLA Ops:
  10.0 6.4 all_gather.31
  16.4 1.1 copy.55
  18.0 16.9 %all-gather.7.cloned.1.call-done = bf16[128,8192]{1,0:T(8,128)(2,1)} async-done(((bf16[128,2048]{1,0:T(8,128)(2,1)}), bf16[128,8192]{1,0:T(8,128)(2,1)}) %all-gather.7.cloned.1.call-update) | async-done | bytes 2097168 | tf_op jit(solution)/shard_map/all_gather | solution.py:60
  34.9 2.1 fusion.1
  36.9 2.2 fusion.3
  39.1 47.0 %all-gather.13.cloned.1.call-done = bf16[8192,128]{1,0:T(8,128)(2,1)} async-done(((bf16[1024,128]{1,0:T(8,128)(2,1)}), bf16[8192,128]{1,0:T(8,128)(2,1)}) %all-gather.13.cloned.1.call-update) | async-done | bytes 2097168 | tf_op jit(solution)/shard_map/all_gather | solution.py:71
  86.1 2.3 fusion.90
  88.4 5.4 all_gather.37
  94.2 41.7 %all-gather.9.cloned.1.call-done = bf16[8192,128]{1,0:T(8,128)(2,1)} async-done(((bf16[1024,128]{1,0:T(8,128)(2,1)}), bf16[8192,128]{1,0:T(8,128)(2,1)}) %all-gather.9.cloned.1.call-update) | async-done | bytes 2097168 | tf_op jit(solution)/shard_map/all_gather | solution.py:70
  135.9 2.3 fusion.89
  138.2 5.8 all_gather.33
  144.7 32.5 %all_gather.34 = bf16[1024,128]{1,0:T(8,128)(2,1)S(1)} all-gather(bf16[128,128]{1,0:T(8,128)(2,1)S(1)} %pad_maximum_fusion.6), channel_id=1, replica_groups=mesh['sweep'=1,'dp'=8,'tensor'=4] {'dp'}, dimensions={0}, use_global_device_ids=true | all-gather | bytes 294912 | tf_op jit(solution)/shard_map/all_gather | solution.py:105
  177.2 34.9 %all-gather = bf16[1024,128,1]{1,0,2:T(8,128)(2,1)} all-gather(bf16[128,128,1]{1,0,2:T(8,128)(2,1)S(1)} %copy.84), channel_id=2, replica_groups=mesh['sweep'=1,'dp'=8,'tensor'=4] {'dp'}, dimensions={0}, use_global_device_ids=true | all-gather | bytes 294912 | tf_op jit(solution)/shard_map/all_gather | solution.py:106
  212.1 155.9 %all-gather.11.cloned.1.call-done = bf16[8192,1024]{1,0:T(8,128)(2,1)} async-done(((bf16[1024,1024]{1,0:T(8,128)(2,1)}), bf16[8192,1024]{1,0:T(8,128)(2,1)}) %all-gather.11.cloned.1.call-update) | async-done | bytes 16777232 | tf_op jit(solution)/shard_map/all_gather | solution.py:69
  368.0 8.1 %convolution_bitcast_fusion = f32[16,8,8,128]{3,1,2,0:T(8,128)S(1)} fusion(bf16[128,8192]{1,0:T(8,128)(2,1)S(1)} %fusion.3, bf16[8192,1024]{1,0:T(8,128)(2,1)} %all-gather.11.cloned.1.call-done), kind=kOutput, calls=%fused_computation.37 | convolution fusion | flops 2147483648 | bytes 19398656 | tf_op jit(solution)/shard_map/dot_general | solution.py:77
  376.6 0.8 fusion.9
  377.4 0.9 fusion.8
  378.3 1.3 fusion.47
  379.6 1.5 fusion.6
  381.1 1.3 copy-done.4
  382.4 1.5 fusion.50
  383.9 2.5 fusion.32
  387.1 4.0 fusion.41
  391.2 56.3 %reduce-scatter.5.cloned.1.call-done = bf16[128,128]{1,0:T(8,128)(2,1)} async-done(((bf16[1024,128]{1,0:T(8,128)(2,1)}), bf16[128,128]{1,0:T(8,128)(2,1)}) %reduce-scatter.5.cloned.1.call-update) | async-done | bytes 32784 | tf_op jit(solution)/shard_map/reduce_scatter | solution.py:145
  447.5 0.8 bitcast_convert_fusion.1
  448.9 1.4 dynamic_update_slice.6
  451.3 13.5 %fusion.91 = f32[128,8192]{1,0:T(8,128)} fusion(bf16[128,1024]{0,1:T(8,128)(2,1)S(1)} %bitcast.168, bf16[8192,1024]{1,0:T(8,128)(2,1)} %all-gather.11.cloned.1.call-done), kind=kOutput, calls=%fused_computation.102 | convolution fusion | flops 2147483648 | bytes 21233664 | tf_op jit(solution)/shard_map/tc,dc->td/dot_general | solution.py:52
  464.8 47.7 %reduce-scatter.9.cloned.1.call-done = bf16[128,128]{1,0:T(8,128)(2,1)} async-done(((bf16[1024,128]{1,0:T(8,128)(2,1)}), bf16[128,128]{1,0:T(8,128)(2,1)}) %reduce-scatter.9.cloned.1.call-update) | async-done | bytes 32784 | tf_op jit(solution)/shard_map/reduce_scatter | solution.py:151
  512.5 0.9 copy.67
  513.4 1.4 dynamic_update_slice.7
  515.6 18.7 %reduce-scatter.7.cloned.1.call-done = bf16[128,128]{0,1:T(8,128)(2,1)} async-done(((bf16[128,512]{0,1:T(8,128)(2,1)}), bf16[128,128]{0,1:T(8,128)(2,1)}) %reduce-scatter.7.cloned.1.call-update) | async-done | bytes 32784 | tf_op jit(solution)/shard_map/reduce_scatter | solution.py:173
  534.2 5.6 convolution_add_fusion.1
  539.8 17.1 %reduce-scatter.11.cloned.1.call-done = bf16[128,128]{0,1:T(8,128)(2,1)} async-done(((bf16[128,512]{0,1:T(8,128)(2,1)}), bf16[128,128]{0,1:T(8,128)(2,1)}) %reduce-scatter.11.cloned.1.call-update) | async-done | bytes 32784 | tf_op jit(solution)/shard_map/reduce_scatter | solution.py:176
  556.9 4.9 fusion
  561.9 0.7 pad_maximum_fusion
  562.7 2.4 copy.81
  565.2 5.5 all-to-all-start
  570.7 42.7 %all-reduce.2.cloned.1.call-done = bf16[128,8192]{1,0:T(8,128)(2,1)} async-done(((bf16[128,8192]{1,0:T(8,128)(2,1)}), bf16[128,8192]{1,0:T(8,128)(2,1)}) %all-reduce.2.cloned.1.call-update) | async-done | bytes 2097168 | tf_op jit(solution)/shard_map/psum | solution.py:195
  613.4 2.2 convert_element_type.142
  615.6 0.8 fusion.4
  616.4 1.4 fusion.58
  617.8 23.2 %psum.15 = f32[2048]{0:T(1024)} all-reduce(f32[2048]{0:T(1024)S(1)} %get-tuple-element.7), channel_id=1, replica_groups=mesh['sweep'=1,'dp'=8,'tensor'=4] {'dp'}, use_global_device_ids=true, to_apply=%region_11.12 | all-reduce | flops 2048 | bytes 16384 | tf_op jit(solution)/shard_map/psum | solution.py:203
  641.0 31.3 %all-gather.15.cloned.1.call-done = bf16[1024,1280]{0,1:T(8,128)(2,1)} async-done(((bf16[128,1280]{0,1:T(8,128)(2,1)}), bf16[1024,1280]{0,1:T(8,128)(2,1)}) %all-gather.15.cloned.1.call-update) | async-done | bytes 2621456 | tf_op jit(solution)/shard_map/all_gather | solution.py:207
  672.4 4.4 copy.69
  676.7 11.9 %convolution_convert_fusion = bf16[8,1024,1280]{2,1,0:T(8,128)(2,1)} fusion(bf16[8,128,1280]{2,1,0:T(8,128)(2,1)} %bitcast.165, bf16[128,8,1024]{0,2,1:T(8,128)(2,1)} %all-to-all-done), kind=kOutput, calls=%fused_computation.1 | convolution fusion | flops 2694840320 | bytes 25690112 | tf_op jit(solution)/shard_map/btd,btc->bdc/dot_general | solution.py:212
  688.7 11.3 %convert_reduce_fusion = f32[1024,1280]{1,0:T(8,128)S(1)} fusion(bf16[8,1024,1280]{2,1,0:T(8,128)(2,1)} %convolution_convert_fusion), kind=kLoop, calls=%fused_computation | loop fusion | flops 19660800 | bytes 26214400 | tf_op jit(solution)/shard_map/reduce_sum | solution.py:213
  699.9 1.0 fusion.87
  701.0 2.7 slice.52
  (71 shorter events, 7.8 us)
Async XLA Ops:
  7.2 27.7 %all-gather.7.cloned.1.call-start = ((), (), s32[]{:S(2)}) async-start(), calls=%async_computation.5 | async-start | bytes 2621440 | tf_op jit(solution)/shard_map/all_gather | solution.py:60
  7.9 78.2 %all-gather.13.cloned.1.call-start = ((), (), s32[]{:S(2)}) async-start(), calls=%async_computation.8 | async-start | bytes 2359296 | tf_op jit(solution)/shard_map/all_gather | solution.py:71
  8.6 127.2 %all-gather.9.cloned.1.call-start = ((), (), s32[]{:S(2)}) async-start(), calls=%async_computation.6 | async-start | bytes 2359296 | tf_op jit(solution)/shard_map/all_gather | solution.py:70
  9.4 358.6 %all-gather.11.cloned.1.call-start = ((), (), s32[]{:S(2)}) async-start(), calls=%async_computation.7 | async-start | bytes 18874368 | tf_op jit(solution)/shard_map/all_gather | solution.py:69
  10.0 437.6 %reduce-scatter.5.cloned.1.call-start = ((), (), s32[]{:S(2)}) async-start(), calls=%async_computation.9 | async-start | bytes 294912 | tf_op jit(solution)/shard_map/reduce_scatter | solution.py:145
  376.6 1.7 copy-start.8
  377.4 2.2 copy-start.1
  378.3 1.3 copy-start.7
  381.1 1.3 copy-start.4
  387.1 125.4 %reduce-scatter.9.cloned.1.call-start = ((), (), s32[]{:S(2)}) async-start(), calls=%async_computation.11 | async-start | bytes 294912 | tf_op jit(solution)/shard_map/reduce_scatter | solution.py:151
  391.2 143.0 %reduce-scatter.7.cloned.1.call-start = ((), (), s32[]{:S(2)}) async-start(), calls=%async_computation.10 | async-start | bytes 163840 | tf_op jit(solution)/shard_map/reduce_scatter | solution.py:173
  450.3 0.7 copy-start.6
  451.0 105.9 %reduce-scatter.11.cloned.1.call-start = ((), (), s32[]{:S(2)}) async-start(), calls=%async_computation.12 | async-start | bytes 163840 | tf_op jit(solution)/shard_map/reduce_scatter | solution.py:176
  514.8 0.7 copy-start.5
  515.5 97.9 %all-reduce.2.cloned.1.call-start = ((), (), s32[]{:S(2)}) async-start(), calls=%async_computation.13 | async-start | bytes 4194304 | tf_op jit(solution)/shard_map/psum | solution.py:195
  539.8 22.1 %copy-start.9 = (bf16[128,128]{0,1:T(8,128)(2,1)S(1)}, bf16[128,128]{0,1:T(8,128)(2,1)}, u32[]{:S(2)}) copy-start(bf16[128,128]{0,1:T(8,128)(2,1)} %reduce-scatter.7.cloned.1.call-done) | copy-start | bytes 98308
  556.9 5.0 copy-start.10
  561.9 110.5 %all-gather.15.cloned.1.call-start = ((), (), s32[]{:S(2)}) async-start(), calls=%async_computation.14 | async-start | bytes 2949120 | tf_op jit(solution)/shard_map/all_gather | solution.py:207
  562.7 8.0 %copy-start.11 = (bf16[2048]{0:T(1024)(128)(2,1)S(1)}, bf16[2048]{0:T(1024)(128)(2,1)}, u32[]{:S(2)}) copy-start(bf16[2048]{0:T(1024)(128)(2,1)} %param.7) | copy-start | bytes 12292
  565.2 111.6 %all-to-all-start = ((bf16[128,8,1024]{0,2,1:T(8,128)(2,1)}), bf16[128,8,1024]{0,2,1:T(8,128)(2,1)}, u32[]{:S(2)}, u32[]{:S(2)}) async-start(bf16[128,8,1024]{0,2,1:T(8,128)(2,1)} %bitcast.166), calls=%async_computation.4 | async-start | bytes 4194304 | tf_op jit(solution)/shard_map/all_to_all | solution.py:206
  570.7 44.9 %copy-start = (bf16[128,8192]{1,0:T(8,128)(2,1)S(1)}, bf16[128,8192]{1,0:T(8,128)(2,1)}, u32[]{:S(2)}) copy-start(bf16[128,8192]{1,0:T(8,128)(2,1)} %all-gather.7.cloned.1.call-done) | copy-start | bytes 6291460
  570.7 45.7 %copy-start.3 = (bf16[128,2048]{1,0:T(8,128)(2,1)S(1)}, bf16[128,2048]{1,0:T(8,128)(2,1)}, u32[]{:S(2)}) copy-start(bf16[128,2048]{1,0:T(8,128)(2,1)} %param.6) | copy-start | bytes 1572868
  613.4 2.2 copy-start.2
Sparse Core Ops, SparseCore 0:
  9.5 25.2 all-gather.6
  37.0 49.0 all-gather.12
  88.2 47.6 all-gather.8
  137.9 230.0 all-gather.10
  387.2 60.2 reduce-scatter.4
  451.3 61.1 reduce-scatter.8
  515.5 18.7 reduce-scatter.6
  537.2 19.6 reduce-scatter.10
  562.0 51.3 all-reduce.1
  615.9 56.4 all-gather.14
where the time goes:
time: 711 us; the launch traced here: 710 us
  waiting for transfers between devices  478 us (67%)
  blocking collectives  108 us (15%)
  matrix products  60.2 us (8%)
  other arithmetic  24.1 us (3%)
  local copies, waits for them, and re-layouts  19.3 us (3%)
  between operations  14.6 us (2%)
    all_gather x1, waiting for transfers between devices, on_device(): lax.all_gather(w_query, 'dp', axis=0, tiled=True)  156 us
    reduce_scatter x1, waiting for transfers between devices, on_device(): lax.psum_scatter(dkey_part.reshape(seq_length, own_kv * head_width).astyp...  56.3 us
    reduce_scatter x1, waiting for transfers between devices, on_device(): lax.psum_scatter(dvalue_part.reshape(seq_length, own_kv * head_width).ast...  47.7 us
    all_gather x1, waiting for transfers between devices, on_device(): lax.all_gather(w_value, 'dp', axis=0, tiled=True)  47 us
    psum x1, waiting for transfers between devices, on_device(): lax.psum(partial_input.astype(jnp.bfloat16), 'tensor').astype(jnp.float32)  42.7 us
    all_gather x1, waiting for transfers between devices, on_device(): lax.all_gather(w_key, 'dp', axis=0, tiled=True)  41.7 us
    all_gather x1, blocking collectives, on_device(): lax.all_gather(value_half, 'dp', axis=0, tiled=True)  34.9 us
    all_gather x1, blocking collectives, on_device(): lax.all_gather(key_rot, 'dp', axis=0, tiled=True)  32.5 us
  transfers between devices with their start and end apart: 11, of which 10 were waited for; matrix products, arithmetic and copies ran while one was open for 7% of the time, Pallas kernels for 0%

commit v1 on v0

v1 whole, which is shorter than its diff:
```python
import functools

import jax
import jax.numpy as jnp
from jax import lax
from jax.experimental import pallas as pl
from jax.experimental.pallas import tpu as pltpu
from jax.sharding import PartitionSpec as P

QHEADS = 32
KVHEADS = 4
HD = 128
EPS = 1e-05
THETA = 500000.0
PAD = 16
MESH = pl.DeviceIdType.MESH
VMEM = pltpu.VMEM


def copy_to(src, dst, send_sem, recv_sem, dp, tensor):
    return pltpu.make_async_remote_copy(
        src_ref=src,
        dst_ref=dst,
        send_sem=send_sem,
        recv_sem=recv_sem,
        device_id={"dp": dp, "tensor": tensor},
        device_id_type=MESH,
    )


def where_am_i():
    return lax.axis_index("dp"), lax.axis_index("tensor")


def meet(ndp, nt):
    dp, tn = where_am_i()
    me, count = dp * nt + tn, ndp * nt
    barrier = pltpu.get_barrier_semaphore()
    for k in range(1, count):
        other = lax.rem(me + k, count)
        pl.semaphore_signal(
            barrier,
            inc=1,
            device_id={"dp": other // nt, "tensor": lax.rem(other, nt)},
            device_id_type=MESH,
        )
    pl.semaphore_wait(barrier, count - 1)


class Sends:
    def __init__(self, sems):
        self.sems, self.used, self.waits = sems, 0, []

    def go(self, src, dst, recv_sem, dp, tensor):
        copy = copy_to(src, dst, self.sems.at[self.used], recv_sem, dp, tensor)
        self.used += 1
        copy.start()
        self.waits.append(copy)

    def finish(self):
        for copy in self.waits:
            copy.wait_send()


def to_everyone(sends, ndp, nt, source, target, recv):
    dp, tn = where_am_i()
    me, count = dp * nt + tn, ndp * nt
    for k in range(1, count):
        other = lax.rem(me + k, count)
        odp, otn = other // nt, lax.rem(other, nt)
        sends.go(source(odp, otn), target, recv.at[me], odp, otn)


def from_everyone(ndp, nt, slot, recv, send_sem):
    dp, tn = where_am_i()
    me, count = dp * nt + tn, ndp * nt
    for k in range(1, count):
        other = lax.rem(me + count - k, count)
        odp, otn = other // nt, lax.rem(other, nt)
        copy_to(slot(odp, otn), slot(odp, otn), send_sem, recv.at[other], odp, otn).wait_recv()


def gather_start(sends, ndp, source, out, recv):
    dp, tn = where_am_i()
    outer, inner, no = dp // 2, lax.rem(dp, 2), ndp // 2
    for k in range(1, no):
        sends.go(source, out.at[dp], recv.at[dp], lax.rem(outer + k, no) * 2 + inner, tn)
    sends.go(source, out.at[dp], recv.at[dp], outer * 2 + 1 - inner, tn)


def gather_finish(sends, ndp, out, recv):
    dp, tn = where_am_i()
    outer, inner, no = dp // 2, lax.rem(dp, 2), ndp // 2
    partner = outer * 2 + 1 - inner
    for k in range(1, no):
        slot = lax.rem(outer + no - k, no) * 2 + inner
        copy_to(out.at[slot], out.at[slot], sends.sems.at[0], recv.at[slot], slot, tn).wait_recv()
        sends.go(out.at[slot], out.at[slot], recv.at[slot], partner, tn)
    for k in range(no):
        slot = lax.rem(outer + no - k, no) * 2 + 1 - inner
        copy_to(out.at[slot], out.at[slot], sends.sems.at[0], recv.at[slot], partner, tn).wait_recv()


def swap_dp(sends, ndp, source, out, recv):
    dp, tn = where_am_i()
    for k in range(1, ndp):
        other = lax.rem(dp + k, ndp)
        sends.go(source.at[other], out.at[dp], recv.at[dp], other, tn)


def swap_dp_finish(sends, ndp, out, recv):
    dp, tn = where_am_i()
    for k in range(1, ndp):
        other = lax.rem(dp + ndp - k, ndp)
        copy_to(out.at[other], out.at[other], sends.sems.at[0], recv.at[other], other, tn).wait_recv()


def spread_kernel(ndp, nt, x_ref, ss_ref, x_out, ss_out, local, ssem, xrecv, srecv):
    dp, tn = where_am_i()
    per = ndp // nt
    meet(ndp, nt)
    sends = Sends(ssem)
    own = pltpu.make_async_copy(ss_ref, ss_out.at[dp, tn], local.at[0])
    own.start()
    firsts = []
    for s in range(per):
        target, relay = tn * per + s, lax.rem(dp, nt)
        mine = jnp.logical_and(target == dp, relay == tn)
        copy = copy_to(x_ref.at[s], x_out.at[dp], ssem.at[sends.used], xrecv.at[dp], target, relay)
        sends.used += 1
        here = pltpu.make_async_copy(x_ref.at[s], x_out.at[dp], local.at[1])

        @pl.when(mine)
        def _():
            here.start()
            here.wait()

        @pl.when(jnp.logical_not(mine))
        def _():
            copy.start()

        firsts.append((mine, copy))
    to_everyone(sends, ndp, nt, lambda a, b: ss_ref, ss_out.at[dp, tn], srecv)
    outer, inner, no = tn // 2, lax.rem(tn, 2), nt // 2
    partner = outer * 2 + 1 - inner
    for m in range(per):
        slot = m * nt + tn
        block = x_out.at[slot]
        mine = jnp.logical_and(slot == dp, dp // per == tn)

        @pl.when(jnp.logical_not(mine))
        def _():
            copy_to(block, block, ssem.at[0], xrecv.at[slot], slot, dp // per).wait_recv()

        for k in range(1, no):
            sends.go(block, block, xrecv.at[slot], dp, lax.rem(outer + k, no) * 2 + inner)
        sends.go(block, block, xrecv.at[slot], dp, partner)
    for k in range(1, no):
        for m in range(per):
            slot = m * nt + lax.rem(outer + no - k, no) * 2 + inner
            block = x_out.at[slot]
            copy_to(block, block, ssem.at[0], xrecv.at[slot], dp, partner).wait_recv()
            sends.go(block, block, xrecv.at[slot], dp, partner)
    for k in range(no):
        for m in range(per):
            slot = m * nt + lax.rem(outer + no - k, no) * 2 + 1 - inner
            block = x_out.at[slot]
            copy_to(block, block, ssem.at[0], xrecv.at[slot], dp, partner).wait_recv()
    from_everyone(ndp, nt, lambda a, b: ss_out.at[a, b], srecv, ssem.at[0])
    own.wait()
    for mine, copy in firsts:

        @pl.when(jnp.logical_not(mine))
        def _():
            copy.wait_send()

    sends.finish()


def forward_kernel(ndp, nt, q_ref, kv_ref, q_out, kv_out, local, ssem, qrecv, kvrecv):
    dp, tn = where_am_i()
    meet(ndp, nt)
    sends = Sends(ssem)
    kv_own = pltpu.make_async_copy(kv_ref.at[tn * KVHEADS // nt, dp], kv_out.at[dp, tn], local.at[0])
    q_own = pltpu.make_async_copy(q_ref.at[dp], q_out.at[dp], local.at[1])
    kv_own.start()
    q_own.start()
    to_everyone(
        sends, ndp, nt, lambda a, b: kv_ref.at[b * KVHEADS // nt, a], kv_out.at[dp, tn], kvrecv
    )
    swap_dp(sends, ndp, q_ref, q_out, qrecv)
    from_everyone(ndp, nt, lambda a, b: kv_out.at[a, b], kvrecv, ssem.at[0])
    swap_dp_finish(sends, ndp, q_out, qrecv)
    kv_own.wait()
    q_own.wait()
    sends.finish()


def gather_kernel(ndp, nt, a_ref, a_out, local, ssem, recv):
    dp, tn = where_am_i()
    meet(ndp, nt)
    sends = Sends(ssem)
    own = pltpu.make_async_copy(a_ref, a_out.at[dp], local.at[0])
    own.start()
    gather_start(sends, ndp, a_ref, a_out, recv)
    gather_finish(sends, ndp, a_out, recv)
    own.wait()
    sends.finish()


def swap_kernel(ndp, nt, a_ref, a_out, local, ssem, recv):
    dp, tn = where_am_i()
    meet(ndp, nt)
    sends = Sends(ssem)
    own = pltpu.make_async_copy(a_ref.at[dp], a_out.at[dp], local.at[0])
    own.start()
    swap_dp(sends, ndp, a_ref, a_out, recv)
    swap_dp_finish(sends, ndp, a_out, recv)
    own.wait()
    sends.finish()


def backward_kernel(ndp, nt, q_ref, kv_ref, q_out, kv_out, local, ssem, qrecv, kvrecv):
    dp, tn = where_am_i()
    meet(ndp, nt)
    sends = Sends(ssem)
    kv_own = pltpu.make_async_copy(kv_ref.at[tn], kv_out.at[dp, tn], local.at[0])
    q_own = pltpu.make_async_copy(q_ref, q_out.at[dp], local.at[1])
    kv_own.start()
    q_own.start()
    to_everyone(sends, ndp, nt, lambda a, b: kv_ref.at[b], kv_out.at[dp, tn], kvrecv)
    gather_start(sends, ndp, q_ref, q_out, qrecv)
    gather_finish(sends, ndp, q_out, qrecv)
    from_everyone(ndp, nt, lambda a, b: kv_out.at[a, b], kvrecv, ssem.at[0])
    kv_own.wait()
    q_own.wait()
    sends.finish()


def tensor_swap_kernel(ndp, nt, a_ref, a_out, local, ssem, recv):
    dp, tn = where_am_i()
    meet(ndp, nt)
    sends = Sends(ssem)
    own = pltpu.make_async_copy(a_ref.at[tn], a_out.at[tn], local.at[0])
    own.start()
    for k in range(1, nt):
        other = lax.rem(tn + k, nt)
        sends.go(a_ref.at[other], a_out.at[tn], recv.at[tn], dp, other)
    for k in range(1, nt):
        other = lax.rem(tn + nt - k, nt)
        copy_to(a_out.at[other], a_out.at[other], ssem.at[0], recv.at[other], dp, other).wait_recv()
    own.wait()
    sends.finish()


def home_kernel(ndp, nt, a_ref, a_out, local, ssem, recv):
    dp, tn = where_am_i()
    per = ndp // nt
    meet(ndp, nt)
    started = []
    for m in range(per):
        target, owner = m * nt + tn, dp // per
        slot = lax.rem(dp, per)
        mine = jnp.logical_and(target == dp, owner == tn)
        copy = copy_to(a_ref.at[m], a_out.at[slot], ssem.at[m], recv.at[slot], target, owner)
        here = pltpu.make_async_copy(a_ref.at[m], a_out.at[slot], local.at[0])

        @pl.when(mine)
        def _():
            here.start()
            here.wait()

        @pl.when(jnp.logical_not(mine))
        def _():
            copy.start()

        started.append((mine, copy))
    for s in range(per):
        source, relay = tn * per + s, lax.rem(dp, nt)
        mine = jnp.logical_and(source == dp, relay == tn)

        @pl.when(jnp.logical_not(mine))
        def _():
            copy_to(a_out.at[s], a_out.at[s], ssem.at[0], recv.at[s], source, relay).wait_recv()

    for mine, copy in started:

        @pl.when(jnp.logical_not(mine))
        def _():
            copy.wait_send()


def last_kernel(ndp, nt, r_ref, g_ref, r_out, g_out, local, ssem, rrecv, grecv):
    dp, tn = where_am_i()
    meet(ndp, nt)
    sends = Sends(ssem)
    r_own = pltpu.make_async_copy(r_ref, r_out.at[tn], local.at[0])
    g_own = pltpu.make_async_copy(g_ref, g_out.at[dp], local.at[1])
    r_own.start()
    g_own.start()
    for k in range(1, nt):
        sends.go(r_ref, r_out.at[tn], rrecv.at[tn], dp, lax.rem(tn + k, nt))
    for k in range(1, ndp):
        sends.go(g_ref, g_out.at[dp], grecv.at[dp], lax.rem(dp + k, ndp), tn)
    for k in range(1, nt):
        other = lax.rem(tn + nt - k, nt)
        copy_to(r_out.at[other], r_out.at[other], ssem.at[0], rrecv.at[other], dp, other).wait_recv()
    swap_dp_finish(sends, ndp, g_out, grecv)
    r_own.wait()
    g_own.wait()
    sends.finish()


def send(kernel, number, ndp, nt, arrays, shapes, sends, recvs):
    dma = pltpu.SemaphoreType.DMA
    many = len(shapes) > 1
    outs = [jax.ShapeDtypeStruct(shape, array.dtype) for shape, array in zip(shapes, arrays)]
    specs = [pl.BlockSpec(memory_space=VMEM)] * len(arrays)
    return pl.pallas_call(
        functools.partial(kernel, ndp, nt),
        out_shape=outs if many else outs[0],
        in_specs=specs,
        out_specs=specs if many else specs[0],
        scratch_shapes=[dma((2,)), dma((sends,))] + [dma((count,)) for count in recvs],
        compiler_params=pltpu.CompilerParams(collective_id=number, has_side_effects=True),
        name=kernel.__name__,
    )(*arrays)


def turn(field, cosine, sine, axis, back):
    front, rear = jnp.split(field, 2, axis)
    sine = -sine if back else sine
    return jnp.concatenate([front * cosine - rear * sine, rear * cosine + front * sine], axis)


def on_device(ndp, nt, checkpoint, norm_gain, w_query, w_key, w_value, grad_attn):
    rows, own_width = checkpoint.shape
    features, q_width = w_query.shape
    k_width = w_key.shape[1]
    entries = k_width // KVHEADS
    width = own_width * nt
    per = ndp // nt
    heads = q_width // HD
    seq = ndp * rows
    everyone = ndp * nt
    f32, bf16 = jnp.float32, jnp.bfloat16
    assert ndp == per * nt and nt % KVHEADS == 0 and heads * nt == QHEADS and features * per == own_width

    x_own = checkpoint.astype(f32)
    squares = jnp.sum(x_own * x_own, -1)
    gain_rows = jnp.broadcast_to(norm_gain.reshape(per, 1, features), (per, PAD, features))
    slices = jnp.concatenate(
        [jnp.transpose(checkpoint.reshape(rows, per, features), (1, 0, 2)), gain_rows], 1
    )
    x_all, squares_all = send(
        spread_kernel,
        1,
        ndp,
        nt,
        (slices, jnp.broadcast_to(squares, (8, rows))),
        ((ndp, rows + PAD, features), (ndp, nt, 8, rows)),
        everyone + 4 * ndp,
        (ndp, everyone),
    )
    inverse_all = lax.rsqrt(jnp.sum(squares_all[:, :, 0], 1) / width + EPS)
    gain = x_all[0, rows].astype(f32)
    normed = (x_all[:, :rows].astype(f32) * inverse_all[:, :, None] * gain).astype(bf16)
    normed = normed.reshape(seq, features)

    q_terms = jnp.dot(normed, w_query, preferred_element_type=f32).astype(bf16)

    def entry_terms(matrix):
        terms = lax.dot_general(matrix, normed, (((0,), (1,)), ((), ())), preferred_element_type=f32)
        return terms.astype(bf16).reshape(entries, KVHEADS, ndp, rows)

    kv_terms = jnp.stack([entry_terms(w_key), entry_terms(w_value)])
    kv_terms = jnp.transpose(kv_terms, (2, 3, 0, 1, 4)).reshape(KVHEADS, ndp, 2 * entries, rows)
    q_parts, kv_parts = send(
        forward_kernel,
        2,
        ndp,
        nt,
        (q_terms.reshape(ndp, rows, q_width), kv_terms),
        ((ndp, rows, q_width), (ndp, nt, 2 * entries, rows)),
        everyone + ndp,
        (ndp, everyone),
    )
    dp = lax.axis_index("dp")
    positions = dp * rows + jnp.arange(rows, dtype=jnp.int32)
    frequency = THETA ** (-(jnp.arange(HD // 2, dtype=f32) * 2.0) / HD)
    angle = positions.astype(f32)[:, None] * frequency[None, :]
    cosine, sine = jnp.cos(angle), jnp.sin(angle)
    cosine_t, sine_t = cosine.T, sine.T
    queries = jnp.sum(q_parts.astype(f32), 0).reshape(rows, heads, HD)
    query_rot = turn(queries, cosine[:, None], sine[:, None], -1, False).astype(bf16)
    kv_sum = jnp.sum(kv_parts.astype(f32), 0).reshape(nt, 2, entries, rows)
    kv_sum = jnp.transpose(kv_sum, (1, 0, 2, 3)).reshape(2, HD, rows)
    key_rot = turn(kv_sum[0], cosine_t, sine_t, 0, False)
    kv_own = jnp.concatenate([key_rot, kv_sum[1]], 0).astype(bf16)
    kv_all = send(
        gather_kernel, 3, ndp, nt, (kv_own,), ((ndp, 2 * HD, rows),), 2 * ndp, (ndp,)
    )
    kv_all = jnp.transpose(kv_all, (1, 0, 2)).reshape(2, HD, seq)
    keys, values = kv_all[0], kv_all[1]

    score_scale = HD ** (-0.5)
    upstream = grad_attn.reshape(rows, heads, HD)
    scores = jnp.einsum("tgd,ds->gts", query_rot, keys, preferred_element_type=f32) * score_scale
    allowed = positions[:, None] >= jnp.arange(seq, dtype=jnp.int32)[None, :]
    scores = jnp.where(allowed, scores, -jnp.inf)
    raw = jnp.exp(scores - jnp.max(scores, -1, keepdims=True))
    chances = raw / jnp.sum(raw, -1, keepdims=True)
    chances_half = chances.astype(bf16)
    attended = jnp.einsum("gts,ds->tgd", chances_half, values, preferred_element_type=f32)
    row_delta = jnp.sum(upstream.astype(f32) * attended, -1)
    prob_grads = jnp.einsum("tgd,ds->gts", upstream, values, preferred_element_type=f32)
    dscore = (chances * (prob_grads - row_delta.T[..., None])).astype(bf16)
    dquery = jnp.einsum("gts,ds->tgd", dscore, keys, preferred_element_type=f32) * score_scale
    dkey = jnp.einsum("gts,tgd->ds", dscore, query_rot, preferred_element_type=f32) * score_scale
    dvalue = jnp.einsum("gts,tgd->ds", chances_half, upstream, preferred_element_type=f32)
    dkv = jnp.concatenate([dkey, dvalue], 0).astype(bf16).reshape(2 * HD, ndp, rows)
    dkv_parts = send(
        swap_kernel,
        4,
        ndp,
        nt,
        (jnp.transpose(dkv, (1, 0, 2)),),
        ((ndp, 2 * HD, rows),),
        ndp,
        (ndp,),
    )
    dkv_sum = jnp.sum(dkv_parts.astype(f32), 0)
    dkv_own = jnp.stack([turn(dkv_sum[:HD], cosine_t, sine_t, 0, True), dkv_sum[HD:]])
    dkv_own = dkv_own.astype(bf16).reshape(2, nt, entries, rows)
    dkv_own = jnp.transpose(dkv_own, (1, 0, 2, 3)).reshape(nt, 2 * entries, rows)
    dquery_pre = turn(dquery, cosine[:, None], sine[:, None], -1, True).astype(bf16)
    dq_all, dkv_all = send(
        backward_kernel,
        5,
        ndp,
        nt,
        (dquery_pre.reshape(rows, q_width), dkv_own),
        ((ndp, rows, q_width), (ndp, nt, 2 * entries, rows)),
        everyone + 2 * ndp,
        (ndp, everyone),
    )
    dq_all = dq_all.reshape(seq, q_width)
    dkv_all = dkv_all.reshape(ndp, KVHEADS, nt // KVHEADS, 2, entries, rows)
    dkv_all = jnp.sum(dkv_all.astype(f32), 2).astype(bf16)
    dkv_all = jnp.transpose(dkv_all, (2, 3, 1, 0, 4)).reshape(2, k_width, seq)

    def cols_back(matrix, grads):
        return lax.dot_general(grads, matrix, (((0,), (1,)), ((), ())), preferred_element_type=f32)

    partial = lax.dot_general(dq_all, w_query, (((1,), (1,)), ((), ())), preferred_element_type=f32)
    partial = partial + cols_back(w_key, dkv_all[0]) + cols_back(w_value, dkv_all[1])
    partial = partial.astype(bf16).reshape(per, nt, rows, features)
    swapped = send(
        tensor_swap_kernel,
        6,
        ndp,
        nt,
        (jnp.transpose(partial, (1, 0, 2, 3)),),
        ((nt, per, rows, features),),
        nt,
        (nt,),
    )
    summed = jnp.sum(swapped.astype(f32), 0).astype(bf16)
    homed = send(home_kernel, 7, ndp, nt, (summed,), ((per, rows, features),), per, (per,))
    dnormed = jnp.transpose(homed, (1, 0, 2)).reshape(rows, own_width).astype(f32)
    gain_own = norm_gain.astype(f32)
    inverse = lax.dynamic_index_in_dim(inverse_all, dp, 0, False)[:, None]
    row_part = jnp.sum(gain_own * dnormed * x_own, -1)
    gain_part = jnp.sum(dnormed * x_own * inverse, 0).reshape(-1, 128)
    row_parts, gain_parts = send(
        last_kernel,
        8,
        ndp,
        nt,
        (jnp.broadcast_to(row_part, (8, rows)), gain_part),
        ((nt, 8, rows), (ndp,) + gain_part.shape),
        ndp + nt,
        (nt, ndp),
    )
    row_sum = jnp.sum(row_parts[:, 0], 0)[:, None]
    d_checkpoint = (
        inverse * gain_own * dnormed - x_own * inverse**3 * row_sum / width
    ).astype(bf16)
    grad_gain = jnp.sum(gain_parts, 0).reshape(own_width)

    def weight_grad(grads, axis):
        return lax.dot_general(
            normed, grads, (((0,), (axis,)), ((), ())), preferred_element_type=f32
        )

    grad_query = weight_grad(dq_all, 0)
    grad_key = weight_grad(dkv_all[0], 1)
    grad_value = weight_grad(dkv_all[1], 1)
    return (d_checkpoint, grad_gain, grad_query, grad_key, grad_value)


def solution(mesh):
    tokens = P(("sweep", "dp"), "tensor")
    gains = P(("sweep", "tensor"))
    return jax.shard_map(
        functools.partial(on_device, mesh.shape["dp"], mesh.shape["tensor"]),
        mesh=mesh,
        in_specs=(tokens, gains, tokens, tokens, tokens, tokens),
        out_specs=(tokens, gains, tokens, tokens, tokens),
        check_vma=False,
    )
```

time: 711 us -> 371 us (0.52)
  waiting for transfers between devices: 478 us -> 0 us
  Pallas kernels: 0 us -> 270 us
  blocking collectives: 108 us -> 0 us
  matrix products: 60.2 us -> 36.5 us
  between operations: 14.6 us -> 1.08 us
  local copies, waits for them, and re-layouts: 19.3 us -> 29.1 us
  other arithmetic: 24.1 us -> 32.6 us
    all_gather x5 -> x0, waiting for transfers between devices: 293 us -> none  [the longest x1 156 us: on_device(): lax.all_gather(w_query, 'dp', axis=0, tiled=True)]
    pallas_call x0 -> x8, Pallas kernels: none -> 270 us  [send(): pl.pallas_call(functools.partial(kernel, ndp, nt), out_shape=outs if many...]
    reduce_scatter x4 -> x0, waiting for transfers between devices: 140 us -> none  [the longest x1 56.3 us: on_device(): lax.psum_scatter(dkey_part.reshape(seq_length, own_kv * head_width).astyp...]
    all_gather x5 -> x0, blocking collectives: 85 us -> none  [the longest x1 34.9 us: on_device(): lax.all_gather(value_half, 'dp', axis=0, tiled=True)]
    psum x1 -> x0, waiting for transfers between devices: 42.7 us -> none  [on_device(): lax.psum(partial_input.astype(jnp.bfloat16), 'tensor').astype(jnp.float32)]
    dot_general x13 -> x14, matrix products: 60.2 us -> 31.9 us  [the longest x3 9.84 us: weight_grad(): lax.dot_general(normed, grads, (((0,), (axis,)), ((), ())), preferred_ele...]
    psum x1 -> x0, blocking collectives: 23.2 us -> none  [on_device(): grad_gain = lax.psum(jnp.sum(input_own * x_own * inverse, 0), 'dp')]
    unnamed x26 -> x41, local copies, waits for them, and re-layouts: 2.93 us -> 13 us
  transfers between devices with their start and end apart: 11 -> 0, of which waited for: 10 -> 0; matrix products, arithmetic and copies ran while one was open for 7% -> 0% of each run, Pallas kernels for 0% -> 0%
where the time goes in v1:
time: 371 us; the launch traced here: 369 us
  Pallas kernels  270 us (73%)
  matrix products  36.5 us (10%)
  other arithmetic  32.6 us (9%)
  local copies, waits for them, and re-layouts  29.1 us (8%)
    pallas_call x8, Pallas kernels, send(): pl.pallas_call(functools.partial(kernel, ndp, nt), out_shape=outs if many...  270 us
    unnamed x41, local copies, waits for them, and re-layouts  13 us
    dot_general x3, matrix products, weight_grad(): lax.dot_general(normed, grads, (((0,), (axis,)), ((), ())), preferred_ele...  9.84 us

profile of v1, /device:TPU:0, one launch (start us, length us, event | category | flops | bytes accessed | tf_op | source)
XLA Modules:
  0.0 369.1 jit_solution(5115345241722002918)
XLA Ops:
  0.7 1.5 copy.58
  4.1 39.5 %spread_kernel.1 = (bf16[8,144,1024]{2,1,0:T(8,128)(2,1)}, f32[8,4,8,128]{3,2,1,0:T(8,128)}) custom-call(bf16[2,144,1024]{2,1,0:T(8,128)(2,1)} %pad_maximum_fusion.x_ref, f32[8,128]{1,0:T(8,128)} %broadcast_in_dim.18.ss_ref), custom_call_target="tpu_custom_call" | custom-call | tf_op jit(solution)/shard_map/spread_kernel/pallas_call | solution.py:319
  43.6 0.9 slice_reduce_fusion
  45.3 2.2 multiply_convert_fusion
  47.5 1.3 copy-done.1
  50.4 1.7 copy.105
  52.1 2.3 fusion.15
  54.6 1.1 maximum_bitcast_fusion
  55.8 1.0 copy.63
  56.8 3.7 convolution_convert_fusion
  60.4 63.4 %forward_kernel.1 = (bf16[8,128,1024]{2,1,0:T(8,128)(2,1)}, bf16[8,4,64,128]{3,2,1,0:T(8,128)(2,1)}) custom-call(bf16[8,128,1024]{2,1,0:T(8,128)(2,1)} %bitcast.175, bf16[4,8,64,128]{3,2,1,0:T(8,128)(2,1)} %bitcast.176), custom_call_target="tpu_custom_call" | custom-call | tf_op jit(solution)/shard_map/forward_kernel/pallas_call | solution.py:319
  123.8 2.0 convert_reduce_fusion
  125.8 1.0 copy.65
  126.8 1.9 fusion.59
  128.7 1.1 copy.102
  129.8 2.0 copy.103
  132.6 2.0 subtract_convert_fusion.1
  135.6 31.1 %gather_kernel.1 = bf16[8,256,128]{2,1,0:T(8,128)(2,1)} custom-call(bf16[256,128]{1,0:T(8,128)(2,1)} %pad_maximum_fusion.2.a_ref), custom_call_target="tpu_custom_call" | custom-call | tf_op jit(solution)/shard_map/gather_kernel/pallas_call | solution.py:319
  166.7 1.1 fusion.60
  169.4 4.5 %fusion.62 = (f32[8,128]{1,0:T(8,128)S(1)}, f32[8,128,1024]{1,2,0:T(8,128)}) fusion(pred[128,1024]{0,1:T(8,128)(4,1)S(1)} %iota_compare_fusion, bf16[128,1024,1]{0,1,2:T(8,128)(2,1)} %bitcast.189, bf16[128,8,64]{2,0,1:T(8,128)(2,1)} %get-tuple-element.36, bf16[128,8,64]{2,0,1:T(8,128)(2,1)} %get-tuple-element.35), kind=kOutput, calls=%fused_computation.115 | convolution fusion | flops 273155072 | bytes 4853760 | tf_op jit(solution)/shard_map/sub | solution.py:411
  174.0 3.8 %fusion.7 = bf16[8,128,1024]{1,2,0:T(8,128)(2,1)} fusion(f32[8,128,1024]{1,2,0:T(8,128)} %get-tuple-element.55, f32[8,128]{1,0:T(8,128)S(1)} %get-tuple-element.54), kind=kLoop, calls=%fused_computation.21 | loop fusion | flops 2097152 | bytes 6295552 | tf_op jit(solution)/shard_map/convert_element_type | solution.py:413
  178.0 1.1 copy.69
  179.1 2.1 fusion.13
  181.2 3.0 fusion.2
  184.3 1.3 copy-done.4
  185.6 1.7 fusion.12
  187.3 1.1 copy.79
  189.3 2.3 fusion.11
  191.8 1.8 maximum_bitcast_fusion.1.a_ref
  193.6 15.2 %swap_kernel.1 = bf16[8,256,128]{2,1,0:T(8,128)(2,1)} custom-call(bf16[8,256,128]{2,1,0:T(8,128)(2,1)} %maximum_bitcast_fusion.1.a_ref), custom_call_target="tpu_custom_call" | custom-call | tf_op jit(solution)/shard_map/swap_kernel/pallas_call | solution.py:319
  208.8 1.1 convert_reduce_fusion.1
  210.8 2.5 fusion.10
  214.4 53.9 %backward_kernel.1 = (bf16[8,128,1024]{2,1,0:T(8,128)(2,1)}, bf16[8,4,64,128]{3,2,1,0:T(8,128)(2,1)}) custom-call(bf16[128,1024]{1,0:T(8,128)(2,1)} %copy_bitcast_fusion.2.q_ref, bf16[4,64,128]{2,1,0:T(8,128)(2,1)} %bitcast.194), custom_call_target="tpu_custom_call" | custom-call | tf_op jit(solution)/shard_map/backward_kernel/pallas_call | solution.py:319
  268.3 1.4 copy.129
  271.3 2.4 fusion.63
  274.4 1.6 copy.128
  276.1 34.3 %tensor_swap_kernel.1 = bf16[4,2,128,1024]{3,2,1,0:T(8,128)(2,1)} custom-call(bf16[4,2,128,1024]{3,2,1,0:T(8,128)(2,1)} %bitcast.166), custom_call_target="tpu_custom_call" | custom-call | tf_op jit(solution)/shard_map/tensor_swap_kernel/pallas_call | solution.py:319
  310.4 2.9 reduce_sum.122.a_ref
  313.3 10.1 %home_kernel.1 = bf16[2,128,1024]{2,1,0:T(8,128)(2,1)} custom-call(bf16[2,128,1024]{2,1,0:T(8,128)(2,1)} %reduce_sum.122.a_ref), custom_call_target="tpu_custom_call" | custom-call | tf_op jit(solution)/shard_map/home_kernel/pallas_call | solution.py:319
  323.5 2.1 convert_bitcast_fusion
  325.6 2.5 copy.87
  328.2 2.5 fusion.23
  331.2 22.2 %last_kernel.1 = (f32[4,8,128]{2,1,0:T(8,128)}, f32[8,16,128]{2,1,0:T(8,128)}) custom-call(f32[8,128]{1,0:T(8,128)} %broadcast_in_dim.21.r_ref, f32[16,128]{1,0:T(8,128)} %bitcast.198), custom_call_target="tpu_custom_call" | custom-call | tf_op jit(solution)/shard_map/last_kernel/pallas_call | solution.py:319
  354.2 2.4 fusion.20
  356.6 2.0 copy.89
  359.2 6.8 %convolution_bitcast_fusion = f32[1024,1024]{1,0:T(8,128)} fusion(bf16[8,128,1024]{2,1,0:T(8,128)(2,1)} %copy-done.1, bf16[8,128,1024]{2,1,0:T(8,128)(2,1)} %get-tuple-element.17), kind=kOutput, calls=%fused_computation.10 | convolution fusion | flops 2147483648 | bytes 8388608 | tf_op jit(solution)/shard_map/dot_general | solution.py:492
  366.0 1.5 fusion.26
  367.5 1.5 fusion.29
  (71 shorter events, 15.4 us)
Async XLA Ops:
  0.6 56.1 %copy-start = (bf16[1024,1024]{1,0:T(8,128)(2,1)S(1)}, bf16[1024,1024]{1,0:T(8,128)(2,1)}, u32[]{:S(2)}) copy-start(bf16[1024,1024]{1,0:T(8,128)(2,1)} %param.8) | copy-start | bytes 6291460
  0.6 1.7 copy-start.13
  45.3 3.5 copy-start.5
  47.5 1.4 copy-start.1
  47.5 4.6 %copy-start.6 = (bf16[1024,128]{1,0:T(8,128)(2,1)S(1)}, bf16[1024,128]{1,0:T(8,128)(2,1)}, u32[]{:S(2)}) copy-start(bf16[1024,128]{1,0:T(8,128)(2,1)} %param.10) | copy-start | bytes 786436
  54.6 2.2 copy-start.2
  131.8 2.8 copy-start.11
  174.0 3.8 %copy-start.14 = (f32[8,128]{1,0:T(8,128)}, f32[8,128]{1,0:T(8,128)S(1)}, u32[]{:S(2)}) copy-start(f32[8,128]{1,0:T(8,128)S(1)} %get-tuple-element.54) | copy-start | bytes 12292
  179.1 2.1 copy-start.15
  181.2 4.3 %copy-start.9 = (bf16[128,8,64]{2,0,1:T(8,128)(2,1)S(1)}, bf16[128,8,64]{2,0,1:T(8,128)(2,1)}, u32[]{:S(2)}) copy-start(bf16[128,8,64]{2,0,1:T(8,128)(2,1)} %get-tuple-element.35) | copy-start | bytes 393220
  181.2 4.3 %copy-start.10 = (bf16[128,8,64]{2,0,1:T(8,128)(2,1)S(1)}, bf16[128,8,64]{2,0,1:T(8,128)(2,1)}, u32[]{:S(2)}) copy-start(bf16[128,8,64]{2,0,1:T(8,128)(2,1)} %get-tuple-element.36) | copy-start | bytes 393220
  184.2 1.3 copy-start.4
  191.8 19.0 %copy-start.8 = (bf16[128,8,128]{0,2,1:T(8,128)(2,1)S(1)}, bf16[128,8,128]{0,2,1:T(8,128)(2,1)}, u32[]{:S(2)}) copy-start(bf16[128,8,128]{0,2,1:T(8,128)(2,1)} %copy.64) | copy-start | bytes 786436
  269.7 1.6 copy-start.16
  271.3 2.4 copy-start.7
  353.4 5.2 %copy-start.12 = (f32[8,16,128]{2,1,0:T(8,128)S(1)}, f32[8,16,128]{2,1,0:T(8,128)}, u32[]{:S(2)}) copy-start(f32[8,16,128]{2,1,0:T(8,128)} %get-tuple-element.20) | copy-start | bytes 196612
  359.2 6.8 %copy-start.3 = (bf16[8,128,1024]{2,1,0:T(8,128)(2,1)S(1)}, bf16[8,128,1024]{2,1,0:T(8,128)(2,1)}, u32[]{:S(2)}) copy-start(bf16[8,128,1024]{2,1,0:T(8,128)(2,1)} %copy-done.1) | copy-start | bytes 6291460
